TPU v7x, 32 devices: a 4x4x1 block of a 4x4x8 slice. The times are simulated.
32 devices in a mesh: dp: 2 (over z, core), tp: 16 (over x, y).
Axes of the slice: x: 4, y: 4, z: 1, core: 2. Of those that a mesh axis runs over, the one named last changes fastest.
The devices are a block of a 4x4x8 slice.
Arguments:
- x: bfloat16 [4096, 7168], P('dp'), parts along dimension 0
- w_gate: bfloat16 [7168, 18432], P(None, 'tp')
- w_up: bfloat16 [7168, 18432], P(None, 'tp')
- w_down: bfloat16 [18432, 7168], P('tp')
Outputs:
- output: bfloat16 [4096, 7168], P('dp'), parts along dimension 0
There are 2 independent parts. A program takes and returns all parts, laid end to end along the dimension named above; an argument that names none is the same for every part.
All inputs are finite; a program needn't handle non-finite values.
Results may differ from a plain program's by a relative error of at most 0.016.
Values are sent between devices in bfloat16 or wider.
A program may use at most 768 MiB of HBM per device.

v0:
```python
import jax
import jax.numpy as jnp
from jax import lax
from jax.sharding import PartitionSpec as P


def solution(mesh):
    def step(x, w_gate, w_up, w_down):
        gate = jnp.dot(x, w_gate, preferred_element_type=jnp.float32)
        up = jnp.dot(x, w_up, preferred_element_type=jnp.float32)
        hidden = (jax.nn.silu(gate) * up).astype(jnp.bfloat16)
        term = jnp.dot(hidden, w_down, preferred_element_type=jnp.float32).astype(jnp.bfloat16)
        return lax.psum(term, "tp")

    return jax.shard_map(
        step,
        mesh=mesh,
        in_specs=(P("dp", None), P(None, "tp"), P(None, "tp"), P("tp", None)),
        out_specs=P("dp", None),
        check_vma=False,
    )
```

profile of v0, /device:TPU:97, one launch (start us, length us, event | category | flops | bytes accessed | tf_op | source)
XLA Modules:
  0.0 512.1 jit_solution(14536612076708161549)
XLA Ops:
  6.5 0.0 all-reduce.2.cloned.1.call-start
  6.6 44.9 %fusion.1 = f32[2048,1152]{1,0:T(8,128)S(1)} fusion(bf16[2048,7168]{1,0:T(8,128)(2,1)} %param.4, bf16[7168,1152]{1,0:T(8,128)(2,1)} %param.5), kind=kOutput, calls=%fused_computation.3 | convolution fusion | flops 33822867456 | bytes 55312384 | tf_op jit(solution)/shard_map/dot_general | solution.py:9
  51.4 47.8 %fusion = bf16[2048,1152]{1,0:T(8,128)(2,1)} fusion(bf16[2048,7168]{1,0:T(8,128)(2,1)} %param.4, bf16[7168,1152]{1,0:T(8,128)(2,1)} %param.6, f32[2048,1152]{1,0:T(8,128)S(1)} %fusion.1), kind=kOutput, calls=%fused_computation.2 | convolution fusion | flops 33837023232 | bytes 60030976 | tf_op jit(solution)/shard_map/dot_general | solution.py:10
  99.2 45.5 %convolution_convert_fusion = bf16[2048,7168]{1,0:T(8,128)(2,1)} fusion(bf16[2048,1152]{1,0:T(8,128)(2,1)} %fusion, bf16[1152,7168]{1,0:T(8,128)(2,1)} %param.7), kind=kOutput, calls=%fused_computation | convolution fusion | flops 33837547520 | bytes 50593792 | tf_op jit(solution)/shard_map/dot_general | solution.py:12
  144.8 0.1 all-reduce.2.cloned.1.call-update
  144.8 340.3 %all-reduce.2.cloned.1.call-done = bf16[2048,7168]{1,0:T(8,128)(2,1)} async-done(((bf16[2048,7168]{1,0:T(8,128)(2,1)}), bf16[2048,7168]{1,0:T(8,128)(2,1)}) %all-reduce.2.cloned.1.call-update) | async-done | bytes 29360144 | tf_op jit(solution)/shard_map/psum | solution.py:13
  485.1 20.1 %copy.6 = bf16[2048,7168]{1,0:T(8,128)(2,1)} copy(bf16[2048,7168]{1,0:T(8,128)(2,1)} %all-reduce.2.cloned.1.call-done) | data formatting | bytes 58720256
Async XLA Ops:
  6.5 478.6 %all-reduce.2.cloned.1.call-start = ((), (), s32[]{:S(2)}) async-start(), calls=%async_computation | async-start | bytes 58720256 | tf_op jit(solution)/shard_map/psum | solution.py:13
Sparse Core Ops, SparseCore 0:
  145.0 340.1 all-reduce.1
where the time goes:
time: 512 us
  waiting for transfers between devices  340 us (66%)
  matrix products  138 us (27%)
  local copies, waits for them, and re-layouts  20.1 us (4%)
  between operations  13.4 us (3%)
    psum x1, waiting for transfers between devices, step(): return lax.psum(term, 'tp')  340 us
    dot_general x1, matrix products, step(): up = jnp.dot(x, w_up, preferred_element_type=jnp.float32)  47.8 us
    dot_general x1, matrix products, step(): jnp.dot(hidden, w_down, preferred_element_type=jnp.float32)  45.5 us
    dot_general x1, matrix products, step(): gate = jnp.dot(x, w_gate, preferred_element_type=jnp.float32)  44.9 us
    unnamed x1, local copies, waits for them, and re-layouts  20.1 us
  transfers between devices with their start and end apart: 1, of which 1 were waited for; matrix products, arithmetic and copies ran while one was open for 0% of the time, Pallas kernels for 0%

commit v1 on v0

v1 whole, which is shorter than its diff:
```python
import functools
import math

import jax
import jax.numpy as jnp
from jax import lax
from jax.experimental import pallas as pl
from jax.experimental.pallas import tpu as pltpu
from jax.sharding import PartitionSpec as P

F32 = jnp.float32
BF16 = jnp.bfloat16

CHUNK = 256
STREAMS = 8
TILE = 128
GU_SLOTS = 3
DN_SLOTS = 3


def kernel(
    side,
    x_hbm, wg_hbm, wu_hbm, wd_hbm, y_hbm,
    x_buf, gu_buf, dn_buf, hidden, part, xred, out1, in1, out2, in2, fin,
    x_sem, gu_sem, dn_sem, fin_sem,
    send1, recv1, send2, recv2, send3, recv3, send4, recv4,
):
    rows, depth = x_hbm.shape
    width = wd_hbm.shape[1] // STREAMS
    ff = wg_hbm.shape[1]
    chunks = rows // CHUNK
    piece = CHUNK // side
    sub = piece // side
    steps = side - 1
    gu_units = ff // TILE
    units = gu_units + STREAMS
    slots = steps * 8

    me = lax.axis_index("tp")
    px, py = me // side, me % side

    def place(stream):
        colour = stream % 4
        first_x = 1 - colour // 2
        d = 1 - 2 * (colour % 2)
        along_x = ((px + d + side) % side) * side + py
        along_y = px * side + (py + d + side) % side
        p1 = first_x * px + (1 - first_x) * py
        p2 = first_x * py + (1 - first_x) * px
        n1 = first_x * along_x + (1 - first_x) * along_y
        n2 = first_x * along_y + (1 - first_x) * along_x
        return d, p1, p2, n1, n2

    def cols(stream):
        return pl.ds(pl.multiple_of(stream * width, 128), width)

    def y_rows(start, size):
        return pl.ds(pl.multiple_of(start, 16), size)

    def x_copy(j):
        return pltpu.make_async_copy(
            x_hbm.at[pl.ds(pl.multiple_of(j * CHUNK, CHUNK), CHUNK)], x_buf.at[j % 2], x_sem.at[j % 2]
        )

    def gu_copies(g):
        src = pl.ds(pl.multiple_of((g % gu_units) * TILE, TILE), TILE)
        slot = g % GU_SLOTS
        return (
            pltpu.make_async_copy(wg_hbm.at[:, src], gu_buf.at[slot, :, pl.ds(0, TILE)], gu_sem.at[slot, 0]),
            pltpu.make_async_copy(wu_hbm.at[:, src], gu_buf.at[slot, :, pl.ds(TILE, TILE)], gu_sem.at[slot, 1]),
        )

    def dn_copy(g):
        slot = g % DN_SLOTS
        return pltpu.make_async_copy(wd_hbm.at[:, cols(g % STREAMS)], dn_buf.at[slot], dn_sem.at[slot])

    def unit(j, u):
        @pl.when(u < gu_units)
        def _():
            g = j * gu_units + u

            @pl.when(u == 0)
            def _():
                x_copy(j).wait()

            for c in gu_copies(g):
                c.wait()
            both = jnp.dot(x_buf[j % 2], gu_buf[g % GU_SLOTS], preferred_element_type=F32)
            gate, up = both[:, :TILE], both[:, TILE:]
            hidden[u] = (jax.nn.silu(gate) * up).astype(BF16)

            @pl.when(g + GU_SLOTS < chunks * gu_units)
            def _():
                for c in gu_copies(g + GU_SLOTS):
                    c.start()

            @pl.when((u == gu_units - 1) & (j + 2 < chunks))
            def _():
                x_copy(j + 2).start()

        @pl.when(u >= gu_units)
        def _():
            s = u - gu_units
            g = j * STREAMS + s
            dn_copy(g).wait()
            h = jnp.concatenate([hidden[i] for i in range(gu_units)], axis=1)
            part[j % 2, s] = jnp.dot(h, dn_buf[g % DN_SLOTS], preferred_element_type=F32)

            @pl.when(g + DN_SLOTS < chunks * STREAMS)
            def _():
                dn_copy(g + DN_SLOTS).start()

    def remote(src, dst, ssem, rsem, to):
        return pltpu.make_async_remote_copy(
            src_ref=src, dst_ref=dst, send_sem=ssem, recv_sem=rsem,
            device_id={"tp": to}, device_id_type=pl.DeviceIdType.MESH,
        )

    def rs1(j, k, s):
        _, _, _, n1, _ = place(s)
        return remote(out1.at[k, s], in1.at[j % 2, k, s], send1.at[k, s], recv1.at[j % 2, k, s], n1)

    def rs2(j, k, s):
        _, _, _, _, n2 = place(s)
        return remote(out2.at[k, s], in2.at[j % 2, k, s], send2.at[k, s], recv2.at[j % 2, k, s], n2)

    def ag2(j, k, s, own):
        d, p1, p2, _, n2 = place(s)
        r = (p2 - d * k + 2 * side) % side
        at = y_hbm.at[y_rows(j * CHUNK + p1 * piece + r * sub, sub), cols(s)]
        return remote(fin.at[s] if own else at, at, send3.at[k, s], recv3.at[j % 2, k, s], n2)

    def ag1(j, k, s):
        d, p1, _, n1, _ = place(s)
        q = (p1 - d * k + 2 * side) % side
        at = y_hbm.at[y_rows(j * CHUNK + q * piece, piece), cols(s)]
        return remote(at, at, send4.at[k, s], recv4.at[j % 2, k, s], n1)

    def fin_copy(j, s):
        _, p1, p2, _, _ = place(s)
        at = y_hbm.at[y_rows(j * CHUNK + p1 * piece + p2 * sub, sub), cols(s)]
        return pltpu.make_async_copy(fin.at[s], at, fin_sem.at[s])

    def each(half, f):
        lax.fori_loop(0, 4, lambda c, _: (f(half * 4 + c), 0)[1], 0)

    def phase1(j, k, half):
        def add(s):
            d, p1, _, _, _ = place(s)
            q = (p1 - d * (1 + k) + 2 * side) % side
            mine = part[j % 2, s, pl.ds(pl.multiple_of(q * piece, piece), piece), :]

            @pl.when(j > 0)
            def _():
                rs1(j - 1, k, s).wait_send()

            @pl.when(k == 0)
            def _():
                out1[0, s] = mine.astype(BF16)

            @pl.when(k > 0)
            def _():
                rs1(j, k - 1, s).wait_recv()
                out1[k, s] = (mine + in1[j % 2, k - 1, s].astype(F32)).astype(BF16)

        each(half, add)
        each(half, lambda s: rs1(j, k, s).start())

    def phase2(j, k, half):
        def add(s):
            d, p1, p2, _, _ = place(s)
            r = (p2 - d * (1 + k) + 2 * side) % side
            at = pl.ds(pl.multiple_of(r * sub, sub), sub)

            @pl.when(j > 0)
            def _():
                rs2(j - 1, k, s).wait_send()

            @pl.when(k == 0)
            def _():
                rs1(j, steps - 1, s).wait_recv()
                mine = part[j % 2, s, pl.ds(pl.multiple_of(p1 * piece, piece), piece), :]
                xred[j % 2, s] = mine + in1[j % 2, steps - 1, s].astype(F32)
                out2[0, s] = xred[j % 2, s, at, :].astype(BF16)

            @pl.when(k > 0)
            def _():
                rs2(j, k - 1, s).wait_recv()
                out2[k, s] = (xred[j % 2, s, at, :] + in2[j % 2, k - 1, s].astype(F32)).astype(BF16)

        each(half, add)
        each(half, lambda s: rs2(j, k, s).start())

    def phase3(j, k, half):
        @pl.when(k == 0)
        def _():
            def add(s):
                _, _, p2, _, _ = place(s)

                @pl.when(j > 0)
                def _():
                    ag2(j - 1, 0, s, True).wait_send()

                rs2(j, steps - 1, s).wait_recv()
                mine = xred[j % 2, s, pl.ds(pl.multiple_of(p2 * sub, sub), sub), :]
                fin[s] = (mine + in2[j % 2, steps - 1, s].astype(F32)).astype(BF16)

            def go(s):
                ag2(j, 0, s, True).start()
                fin_copy(j, s).start()

            each(half, add)
            each(half, go)

        @pl.when(k > 0)
        def _():
            def go(s):
                @pl.when(j > 0)
                def _():
                    ag2(j - 1, k, s, False).wait_send()

                @pl.when(k == 1)
                def _():
                    fin_copy(j, s).wait()

                ag2(j, k - 1, s, False).wait_recv()
                ag2(j, k, s, False).start()

            each(half, go)

    def phase4(j, k, half):
        def go(s):
            @pl.when(j > 0)
            def _():
                ag1(j - 1, k, s).wait_send()

            @pl.when(k == 0)
            def _():
                ag2(j, steps - 1, s, False).wait_recv()

                @pl.when(j > 0)
                def _():
                    ag1(j - 1, steps - 1, s).wait_recv()

            @pl.when(k > 0)
            def _():
                ag1(j, k - 1, s).wait_recv()

            ag1(j, k, s).start()

        each(half, go)

    x_copy(0).start()
    for g in range(GU_SLOTS):
        for c in gu_copies(g):
            c.start()
    for g in range(DN_SLOTS):
        dn_copy(g).start()
    x_copy(1).start()

    barrier = pltpu.get_barrier_semaphore()
    for to in (
        ((px + 1) % side) * side + py,
        ((px + side - 1) % side) * side + py,
        px * side + (py + 1) % side,
        px * side + (py + side - 1) % side,
    ):
        pl.semaphore_signal(barrier, inc=1, device_id={"tp": to}, device_id_type=pl.DeviceIdType.MESH)
    pl.semaphore_wait(barrier, 4)

    def slot(n, carry):
        filling = n < units
        i = jnp.where(filling, 0, n - units)
        t, rest = i // slots, i % slots
        k, m = rest // 8, rest % 8
        half = m % 2
        for phase, f in enumerate((phase1, phase2, phase3, phase4)):
            @pl.when((n >= units) & (m // 2 == phase) & (t >= phase) & (t - phase < chunks))
            def _():
                f(t - phase, k, half)

        u = jnp.where(filling, n, (units * rest) // slots)
        busy = filling | ((units * (rest + 1)) // slots > (units * rest) // slots)
        at = jnp.where(filling, 0, t + 1)

        @pl.when(busy & (at < chunks))
        def _():
            unit(at, u)

        return carry

    lax.fori_loop(0, units + (chunks + 3) * slots, slot, 0)

    last = chunks - 1

    def drain(s, carry):
        ag1(last, steps - 1, s).wait_recv()
        for k in range(steps):
            rs1(last, k, s).wait_send()
            rs2(last, k, s).wait_send()
            ag2(last, k, s, k == 0).wait_send()
            ag1(last, k, s).wait_send()
        return carry

    lax.fori_loop(0, STREAMS, drain, 0)


def solution(mesh):
    tp = mesh.shape["tp"]
    side = math.isqrt(tp)

    def step(x, w_gate, w_up, w_down):
        rows, depth = x.shape
        ff, d_out = w_down.shape
        width = d_out // STREAMS
        piece = CHUNK // side
        sub = piece // side
        steps = side - 1
        any_spec = pl.BlockSpec(memory_space=pl.ANY)
        dma = pltpu.SemaphoreType.DMA
        return pl.pallas_call(
            functools.partial(kernel, side),
            out_shape=jax.ShapeDtypeStruct((rows, d_out), BF16),
            in_specs=[any_spec] * 4,
            out_specs=any_spec,
            scratch_shapes=[
                pltpu.VMEM((2, CHUNK, depth), BF16),
                pltpu.VMEM((GU_SLOTS, depth, 2 * TILE), BF16),
                pltpu.VMEM((DN_SLOTS, ff, width), BF16),
                pltpu.VMEM((ff // TILE, CHUNK, TILE), BF16),
                pltpu.VMEM((2, STREAMS, CHUNK, width), F32),
                pltpu.VMEM((2, STREAMS, piece, width), F32),
                pltpu.VMEM((steps, STREAMS, piece, width), BF16),
                pltpu.VMEM((2, steps, STREAMS, piece, width), BF16),
                pltpu.VMEM((steps, STREAMS, sub, width), BF16),
                pltpu.VMEM((2, steps, STREAMS, sub, width), BF16),
                pltpu.VMEM((STREAMS, sub, width), BF16),
                dma((2,)),
                dma((GU_SLOTS, 2)),
                dma((DN_SLOTS,)),
                dma((STREAMS,)),
            ]
            + [dma((steps, STREAMS)), dma((2, steps, STREAMS))] * 4,
            compiler_params=pltpu.CompilerParams(
                collective_id=0, has_side_effects=True, vmem_limit_bytes=66_000_000
            ),
            cost_estimate=pl.CostEstimate(
                flops=6 * rows * depth * ff, bytes_accessed=8 * 3 * depth * ff * 2, transcendentals=rows * ff
            ),
            name="mlp_ring",
        )(x, w_gate, w_up, w_down)

    return jax.shard_map(
        step,
        mesh=mesh,
        in_specs=(P("dp", None), P(None, "tp"), P(None, "tp"), P("tp", None)),
        out_specs=P("dp", None),
        check_vma=False,
    )
```

time: 512 us -> 368 us (0.72)
  Pallas kernels: 0 us -> 347 us
  waiting for transfers between devices: 340 us -> 0 us
  matrix products: 138 us -> 0 us
  between operations: 13.4 us -> 0.01 us
    pallas_call x0 -> x1, Pallas kernels: none -> 347 us  [step(): pl.pallas_call(functools.partial(kernel, side), out_shape=jax.ShapeDtypeS...]
    psum x1 -> x0, waiting for transfers between devices: 340 us -> none  [step(): return lax.psum(term, 'tp')]
    dot_general x3 -> x0, matrix products: 138 us -> none  [the longest x1 47.8 us: step(): up = jnp.dot(x, w_up, preferred_element_type=jnp.float32)]
  transfers between devices with their start and end apart: 1 -> 0, of which waited for: 1 -> 0; matrix products, arithmetic and copies ran while one was open for 0% -> 0% of each run, Pallas kernels for 0% -> 0%
where the time goes in v1:
time: 368 us; the launch traced here: 367 us
  Pallas kernels  347 us (94%)
  local copies, waits for them, and re-layouts  20.2 us (5%)
    pallas_call x1, Pallas kernels, step(): pl.pallas_call(functools.partial(kernel, side), out_shape=jax.ShapeDtypeS...  347 us
    unnamed x1, local copies, waits for them, and re-layouts  20.2 us

profile of v1, /device:TPU:97, one launch (start us, length us, event | category | flops | bytes accessed | tf_op | source)
XLA Modules:
  0.0 367.4 jit_solution(8217513045270054794)
XLA Ops:
  0.0 347.3 %mlp_ring.1 = bf16[2048,7168]{1,0:T(8,128)(2,1)} custom-call(bf16[2048,7168]{1,0:T(8,128)(2,1)} %x_hbm.1, bf16[7168,1152]{1,0:T(8,128)(2,1)} %wg_hbm.1, bf16[7168,1152]{1,0:T(8,128)(2,1)} %wu_hbm.1, bf16[1152,7168]{1,0:T(8,128)(2,1)} %wd_hbm.1), custom_call_target="tpu_custom_call" | custom-call | flops 101468602368 | bytes 396361728 | tf_op jit(solution)/shard_map/mlp_ring/pallas_call | solution.py:321
  347.3 20.2 %copy.6 = bf16[2048,7168]{1,0:T(8,128)(2,1)} copy(bf16[2048,7168]{1,0:T(8,128)(2,1)} %mlp_ring.1) | data formatting | bytes 58720256

commit v2 on v1

--- a/solution.py
+++ b/solution.py
@@ -14,6 +14,7 @@
 CHUNK = 256
 STREAMS = 8
 TILE = 128
+COPY_FLOPS = 4096
 GU_SLOTS = 3
 DN_SLOTS = 3
 
@@ -52,7 +53,11 @@
         return d, p1, p2, n1, n2
 
     def cols(stream):
-        return pl.ds(pl.multiple_of(stream * width, 128), width)
+        slab = 2 * (stream % 4) + stream // 4
+        return pl.ds(pl.multiple_of(slab * width, 128), width)
+
+    def colour_cols(c):
+        return pl.ds(pl.multiple_of(c * 2 * width, 128), 2 * width)
 
     def y_rows(start, size):
         return pl.ds(pl.multiple_of(start, 16), size)
@@ -98,6 +103,15 @@
             def _():
                 x_copy(j + 2).start()
 
+            @pl.when((j == 0) & (u == gu_units // 2))
+            def _():
+                for i in range(DN_SLOTS):
+                    dn_copy(i).start()
+
+            @pl.when((j == 0) & (u == gu_units - 1))
+            def _():
+                x_copy(1).start()
+
         @pl.when(u >= gu_units)
         def _():
             s = u - gu_units
@@ -120,15 +134,15 @@
         _, _, _, n1, _ = place(s)
         return remote(out1.at[k, s], in1.at[j % 2, k, s], send1.at[k, s], recv1.at[j % 2, k, s], n1)
 
-    def rs2(j, k, s):
-        _, _, _, _, n2 = place(s)
-        return remote(out2.at[k, s], in2.at[j % 2, k, s], send2.at[k, s], recv2.at[j % 2, k, s], n2)
-
-    def ag2(j, k, s, own):
-        d, p1, p2, _, n2 = place(s)
+    def rs2(j, k, c):
+        _, _, _, _, n2 = place(c)
+        return remote(out2.at[k, c], in2.at[j % 2, k, c], send2.at[k, c], recv2.at[j % 2, k, c], n2)
+
+    def ag2(j, k, c, own):
+        d, p1, p2, _, n2 = place(c)
         r = (p2 - d * k + 2 * side) % side
-        at = y_hbm.at[y_rows(j * CHUNK + p1 * piece + r * sub, sub), cols(s)]
-        return remote(fin.at[s] if own else at, at, send3.at[k, s], recv3.at[j % 2, k, s], n2)
+        at = y_hbm.at[y_rows(j * CHUNK + p1 * piece + r * sub, sub), colour_cols(c)]
+        return remote(fin.at[c] if own else at, at, send3.at[k, c], recv3.at[j % 2, k, c], n2)
 
     def ag1(j, k, s):
         d, p1, _, n1, _ = place(s)
@@ -136,15 +150,15 @@
         at = y_hbm.at[y_rows(j * CHUNK + q * piece, piece), cols(s)]
         return remote(at, at, send4.at[k, s], recv4.at[j % 2, k, s], n1)
 
-    def fin_copy(j, s):
-        _, p1, p2, _, _ = place(s)
-        at = y_hbm.at[y_rows(j * CHUNK + p1 * piece + p2 * sub, sub), cols(s)]
-        return pltpu.make_async_copy(fin.at[s], at, fin_sem.at[s])
-
-    def each(half, f):
-        lax.fori_loop(0, 4, lambda c, _: (f(half * 4 + c), 0)[1], 0)
-
-    def phase1(j, k, half):
+    def fin_copy(j, c):
+        _, p1, p2, _, _ = place(c)
+        at = y_hbm.at[y_rows(j * CHUNK + p1 * piece + p2 * sub, sub), colour_cols(c)]
+        return pltpu.make_async_copy(fin.at[c], at, fin_sem.at[c])
+
+    def each(first, count, f):
+        lax.fori_loop(first, first + count, lambda s, _: (f(s), 0)[1], 0)
+
+    def phase1(j, k, first, count):
         def add(s):
             d, p1, _, _, _ = place(s)
             q = (p1 - d * (1 + k) + 2 * side) % side
@@ -163,70 +177,76 @@
                 rs1(j, k - 1, s).wait_recv()
                 out1[k, s] = (mine + in1[j % 2, k - 1, s].astype(F32)).astype(BF16)
 
-        each(half, add)
-        each(half, lambda s: rs1(j, k, s).start())
-
-    def phase2(j, k, half):
-        def add(s):
-            d, p1, p2, _, _ = place(s)
+        each(first, count, add)
+        each(first, count, lambda s: rs1(j, k, s).start())
+
+    def phase2(j, k):
+        def add(c):
+            d, p1, p2, _, _ = place(c)
             r = (p2 - d * (1 + k) + 2 * side) % side
             at = pl.ds(pl.multiple_of(r * sub, sub), sub)
 
             @pl.when(j > 0)
             def _():
-                rs2(j - 1, k, s).wait_send()
+                rs2(j - 1, k, c).wait_send()
 
             @pl.when(k == 0)
             def _():
-                rs1(j, steps - 1, s).wait_recv()
-                mine = part[j % 2, s, pl.ds(pl.multiple_of(p1 * piece, piece), piece), :]
-                xred[j % 2, s] = mine + in1[j % 2, steps - 1, s].astype(F32)
-                out2[0, s] = xred[j % 2, s, at, :].astype(BF16)
+                for h in range(2):
+                    s = 4 * h + c
+                    rs1(j, steps - 1, s).wait_recv()
+                    mine = part[j % 2, s, pl.ds(pl.multiple_of(p1 * piece, piece), piece), :]
+                    xred[j % 2, s] = mine + in1[j % 2, steps - 1, s].astype(F32)
+                    out2[0, c, h] = xred[j % 2, s, at, :].astype(BF16)
 
             @pl.when(k > 0)
             def _():
-                rs2(j, k - 1, s).wait_recv()
-                out2[k, s] = (xred[j % 2, s, at, :] + in2[j % 2, k - 1, s].astype(F32)).astype(BF16)
-
-        each(half, add)
-        each(half, lambda s: rs2(j, k, s).start())
-
-    def phase3(j, k, half):
+                rs2(j, k - 1, c).wait_recv()
+                for h in range(2):
+                    mine = xred[j % 2, 4 * h + c, at, :]
+                    out2[k, c, h] = (mine + in2[j % 2, k - 1, c, h].astype(F32)).astype(BF16)
+
+        each(0, 4, add)
+        each(0, 4, lambda c: rs2(j, k, c).start())
+
+    def phase3(j, k):
         @pl.when(k == 0)
         def _():
-            def add(s):
-                _, _, p2, _, _ = place(s)
+            def add(c):
+                _, _, p2, _, _ = place(c)
 
                 @pl.when(j > 0)
                 def _():
-                    ag2(j - 1, 0, s, True).wait_send()
-
-                rs2(j, steps - 1, s).wait_recv()
-                mine = xred[j % 2, s, pl.ds(pl.multiple_of(p2 * sub, sub), sub), :]
-                fin[s] = (mine + in2[j % 2, steps - 1, s].astype(F32)).astype(BF16)
-
-            def go(s):
-                ag2(j, 0, s, True).start()
-                fin_copy(j, s).start()
-
-            each(half, add)
-            each(half, go)
+                    ag2(j - 1, 0, c, True).wait_send()
+
+                rs2(j, steps - 1, c).wait_recv()
+                for h in range(2):
+                    mine = xred[j % 2, 4 * h + c, pl.ds(pl.multiple_of(p2 * sub, sub), sub), :]
+                    total = mine + in2[j % 2, steps - 1, c, h].astype(F32)
+                    fin[c, :, h * width : (h + 1) * width] = total.astype(BF16)
+
+            def go(c):
+                ag2(j, 0, c, True).start()
+                fin_copy(j, c).start()
+
+            each(0, 4, add)
+            each(0, 4, go)
 
         @pl.when(k > 0)
         def _():
-            def go(s):
+            def go(c):
                 @pl.when(j > 0)
                 def _():
-                    ag2(j - 1, k, s, False).wait_send()
+                    ag2(j - 1, k, c, False).wait_send()
 
                 @pl.when(k == 1)
                 def _():
-                    fin_copy(j, s).wait()
-
-                ag2(j, k - 1, s, False).wait_recv()
-                ag2(j, k, s, False).start()
-
-            each(half, go)
+                    fin_copy(j, c).wait()
+
+                ag2(j, k - 1, c, False).wait_recv()
+                ag2(j, k, c, False).start()
+
+            each(0, 4, go)
 
     def phase4(j, k, half):
         def go(s):
@@ -236,7 +256,9 @@
 
             @pl.when(k == 0)
             def _():
-                ag2(j, steps - 1, s, False).wait_recv()
+                @pl.when(s < 4)
+                def _():
+                    ag2(j, steps - 1, s, False).wait_recv()
 
                 @pl.when(j > 0)
                 def _():
@@ -248,15 +270,12 @@
 
             ag1(j, k, s).start()
 
-        each(half, go)
+        each(4 * half, 4, go)
 
     x_copy(0).start()
     for g in range(GU_SLOTS):
         for c in gu_copies(g):
             c.start()
-    for g in range(DN_SLOTS):
-        dn_copy(g).start()
-    x_copy(1).start()
 
     barrier = pltpu.get_barrier_semaphore()
     for to in (
@@ -268,19 +287,37 @@
         pl.semaphore_signal(barrier, inc=1, device_id={"tp": to}, device_id_type=pl.DeviceIdType.MESH)
     pl.semaphore_wait(barrier, 4)
 
-    def slot(n, carry):
-        filling = n < units
-        i = jnp.where(filling, 0, n - units)
+    last = chunks - 1
+    fill = units + 1
+
+    def turn(n, carry):
+        filling = n < fill
+        i = jnp.where(filling, 0, n - fill)
         t, rest = i // slots, i % slots
         k, m = rest // 8, rest % 8
         half = m % 2
-        for phase, f in enumerate((phase1, phase2, phase3, phase4)):
-            @pl.when((n >= units) & (m // 2 == phase) & (t >= phase) & (t - phase < chunks))
-            def _():
-                f(t - phase, k, half)
+
+        ready = jnp.where(filling, n - 1 - gu_units, 4 * half)
+        again = (n >= fill) & (m < 2) & (t < chunks) & ((t > 0) | (k > 0))
+
+        @pl.when((filling & (n > gu_units)) | again)
+        def _():
+            phase1(t, k, ready, jnp.where(filling, 1, 4))
+
+        @pl.when((n >= fill) & (m == 2) & (t >= 1) & (t - 1 < chunks))
+        def _():
+            phase2(t - 1, k)
+
+        @pl.when((n >= fill) & (m == 4) & (t >= 2) & (t - 2 < chunks))
+        def _():
+            phase3(t - 2, k)
+
+        @pl.when((n >= fill) & (m >= 6) & (t >= 3) & (t - 3 < last))
+        def _():
+            phase4(t - 3, k, half)
 
         u = jnp.where(filling, n, (units * rest) // slots)
-        busy = filling | ((units * (rest + 1)) // slots > (units * rest) // slots)
+        busy = (n < units) | ((n >= fill) & ((units * (rest + 1)) // slots > (units * rest) // slots))
         at = jnp.where(filling, 0, t + 1)
 
         @pl.when(busy & (at < chunks))
@@ -289,20 +326,123 @@
 
         return carry
 
-    lax.fori_loop(0, units + (chunks + 3) * slots, slot, 0)
-
-    last = chunks - 1
+    lax.fori_loop(0, fill + (chunks + 2) * slots, turn, 0)
 
     def drain(s, carry):
-        ag1(last, steps - 1, s).wait_recv()
+        ag1(last - 1, steps - 1, s).wait_recv()
         for k in range(steps):
             rs1(last, k, s).wait_send()
-            rs2(last, k, s).wait_send()
-            ag2(last, k, s, k == 0).wait_send()
-            ag1(last, k, s).wait_send()
+            ag1(last - 1, k, s).wait_send()
         return carry
 
+    def drain2(c, carry):
+        ag2(last, steps - 1, c, False).wait_recv()
+        for k in range(steps):
+            rs2(last, k, c).wait_send()
+            ag2(last, k, c, k == 0).wait_send()
+        return carry
+
     lax.fori_loop(0, STREAMS, drain, 0)
+    lax.fori_loop(0, 4, drain2, 0)
+
+
+def copy_rows(src_ref, *refs):
+    refs[-1][...] = src_ref[...]
+
+
+def copy_into(src, dst, first, count, block):
+    rows, width = src.shape
+    at = first // block
+    spec = pl.BlockSpec((block, width), lambda i: (i + at, 0))
+    return pl.pallas_call(
+        copy_rows,
+        grid=(count // block,),
+        out_shape=jax.ShapeDtypeStruct(src.shape, src.dtype),
+        in_specs=[spec] + ([] if dst is None else [pl.BlockSpec(memory_space=pl.ANY)]),
+        out_specs=spec,
+        input_output_aliases={} if dst is None else {1: 0},
+        compiler_params=pltpu.CompilerParams(vmem_limit_bytes=44 << 20),
+        cost_estimate=pl.CostEstimate(
+            flops=count * width * COPY_FLOPS, bytes_accessed=4 * count * width, transcendentals=0
+        ),
+        name="copy_rows",
+    )(*([src] if dst is None else [src, dst]))
+
+
+def place_pieces(side, n_in, base, *refs):
+    ins, out, sems = refs[:n_in], refs[n_in + 1], refs[n_in + 2]
+    me = lax.axis_index("tp")
+    px, py = me // side, me % side
+    piece = ins[0].shape[0]
+    half, quarter = ins[0].shape[1], ins[0].shape[1] // 2
+    stores = []
+    for axis, p in enumerate((px, py)):
+        for n, (shift, col, w) in enumerate(
+            ((0, 0, half), (side - 1, 0, half), (1, 0, half), (side - 2, 0, quarter), (2, quarter, quarter))
+        ):
+            i = axis * 5 + n
+            at = pl.ds(pl.multiple_of(base + (p + shift) % side * piece, piece), piece)
+            stores.append(
+                pltpu.make_async_copy(ins[i], out.at[at, pl.ds(axis * half + col, w)], sems.at[i])
+            )
+    for store in stores:
+        store.start()
+    for store in stores:
+        store.wait()
+
+
+def finish(side, y, base, pieces):
+    n = len(pieces)
+    any_spec = pl.BlockSpec(memory_space=pl.ANY)
+    return pl.pallas_call(
+        functools.partial(place_pieces, side, n, base),
+        out_shape=jax.ShapeDtypeStruct(y.shape, y.dtype),
+        in_specs=[pl.BlockSpec(memory_space=pltpu.VMEM)] * n + [any_spec],
+        out_specs=any_spec,
+        scratch_shapes=[pltpu.SemaphoreType.DMA((n,))],
+        input_output_aliases={n: 0},
+        compiler_params=pltpu.CompilerParams(vmem_limit_bytes=8 << 20),
+        name="place_pieces",
+    )(*pieces, y)
+
+
+def gather_last(side, y):
+    rows, d_out = y.shape
+    half, quarter, piece, base = d_out // 2, d_out // 4, CHUNK // side, rows - CHUNK
+    me = lax.axis_index("tp")
+    px, py = me // side, me % side
+
+    def ring(dx, dy):
+        grid = [(x, w) for x in range(side) for w in range(side)]
+        return [(x * side + w, (x + dx) % side * side + (w + dy) % side) for x, w in grid]
+
+    pieces = []
+    near, own = [], []
+    for axis, p in enumerate((px, py)):
+        mine = lax.dynamic_slice(y, (base + p * piece, axis * half), (piece, half))
+        own.append(mine)
+    for axis in range(2):
+        step = (1, 0) if axis == 0 else (0, 1)
+        back = (-1, 0) if axis == 0 else (0, -1)
+        near.append((lax.ppermute(own[axis], "tp", ring(*step)), lax.ppermute(own[axis], "tp", ring(*back))))
+    part = base * 5 // 8 // 128 * 128
+    out = copy_into(y, None, 0, part, 128)
+    (near, out) = lax.optimization_barrier((near, out))
+    far = []
+    for axis in range(2):
+        step = (1, 0) if axis == 0 else (0, 1)
+        back = (-1, 0) if axis == 0 else (0, -1)
+        from_back, from_ahead = near[axis]
+        far.append(
+            (
+                lax.ppermute(from_back[:, :quarter], "tp", ring(*step)),
+                lax.ppermute(from_ahead[:, quarter:], "tp", ring(*back)),
+            )
+        )
+    out = copy_into(y, out, part, base - part, 128)
+    for axis in range(2):
+        pieces += [own[axis], *near[axis], *far[axis]]
+    return finish(side, out, base, pieces)
 
 
 def solution(mesh):
@@ -318,7 +458,7 @@
         steps = side - 1
         any_spec = pl.BlockSpec(memory_space=pl.ANY)
         dma = pltpu.SemaphoreType.DMA
-        return pl.pallas_call(
+        y = pl.pallas_call(
             functools.partial(kernel, side),
             out_shape=jax.ShapeDtypeStruct((rows, d_out), BF16),
             in_specs=[any_spec] * 4,
@@ -332,15 +472,15 @@
                 pltpu.VMEM((2, STREAMS, piece, width), F32),
                 pltpu.VMEM((steps, STREAMS, piece, width), BF16),
                 pltpu.VMEM((2, steps, STREAMS, piece, width), BF16),
-                pltpu.VMEM((steps, STREAMS, sub, width), BF16),
-                pltpu.VMEM((2, steps, STREAMS, sub, width), BF16),
-                pltpu.VMEM((STREAMS, sub, width), BF16),
+                pltpu.VMEM((steps, 4, 2, sub, width), BF16),
+                pltpu.VMEM((2, steps, 4, 2, sub, width), BF16),
+                pltpu.VMEM((4, sub, 2 * width), BF16),
                 dma((2,)),
                 dma((GU_SLOTS, 2)),
                 dma((DN_SLOTS,)),
-                dma((STREAMS,)),
+                dma((4,)),
             ]
-            + [dma((steps, STREAMS)), dma((2, steps, STREAMS))] * 4,
+            + [dma((steps, n)) if one else dma((2, steps, n)) for n in (8, 4, 4, 8) for one in (1, 0)],
             compiler_params=pltpu.CompilerParams(
                 collective_id=0, has_side_effects=True, vmem_limit_bytes=66_000_000
             ),
@@ -349,6 +489,7 @@
             ),
             name="mlp_ring",
         )(x, w_gate, w_up, w_down)
+        return gather_last(side, y)
 
     return jax.shard_map(
         step,

time: 368 us -> 364 us (0.989)
  local copies, waits for them, and re-layouts: 20.2 us -> 1.3 us
  starting transfers between devices: 0 us -> 8.87 us
  Pallas kernels: 347 us -> 352 us
    pallas_call x0 -> x3, Pallas kernels: none -> 24 us  [the longest x2 22.1 us: copy_into(): pl.pallas_call(copy_rows, grid=(count // block,), out_shape=jax.ShapeDtyp...]
    unnamed x1 -> x0, local copies, waits for them, and re-layouts: 20.2 us -> none
    pallas_call x1, Pallas kernels: 347 us -> 328 us  [step(): pl.pallas_call(functools.partial(kernel, side), out_shape=jax.ShapeDtypeS...]
    ppermute x0 -> x8, starting transfers between devices: none -> 8.87 us  [the longest x2 4.6 us: gather_last(): lax.ppermute(own[axis], 'tp', ring(*back))]
  transfers between devices with their start and end apart: 0 -> 8, of which waited for: 0 -> 0; matrix products, arithmetic and copies ran while one was open for 0% -> 0% of each run, Pallas kernels for 0% -> 6%
where the time goes in v2:
time: 364 us; the launch traced here: 363 us
  Pallas kernels  352 us (97%)
  starting transfers between devices  8.87 us (2%)
    pallas_call x1, Pallas kernels, step(): pl.pallas_call(functools.partial(kernel, side), out_shape=jax.ShapeDtypeS...  328 us
    pallas_call x2, Pallas kernels, copy_into(): pl.pallas_call(copy_rows, grid=(count // block,), out_shape=jax.ShapeDtyp...  22.1 us
  transfers between devices with their start and end apart: 8, of which 0 were waited for; matrix products, arithmetic and copies ran while one was open for 0% of the time, Pallas kernels for 6%

profile of v2, /device:TPU:97, one launch (start us, length us, event | category | flops | bytes accessed | tf_op | source)
XLA Modules:
  0.0 362.7 jit_solution(790201261447956776)
XLA Ops:
  0.0 328.4 %mlp_ring.1.src_ref = bf16[2048,7168]{1,0:T(8,128)(2,1)} custom-call(bf16[2048,7168]{1,0:T(8,128)(2,1)} %x_hbm.1, bf16[7168,1152]{1,0:T(8,128)(2,1)} %wg_hbm.1, bf16[7168,1152]{1,0:T(8,128)(2,1)} %wu_hbm.1, bf16[1152,7168]{1,0:T(8,128)(2,1)} %wd_hbm.1), custom_call_target="tpu_custom_call" | custom-call | flops 101468602368 | bytes 396361728 | tf_op jit(solution)/shard_map/mlp_ring/pallas_call | solution.py:461
  328.4 1.2 constant_dynamic-slice_fusion
  329.6 3.0 collective-permute-start.3
  332.7 0.0 collective-permute-start.2
  332.7 1.6 collective-permute-start.1
  334.2 0.0 collective-permute-start
  334.2 12.6 %copy_rows.2.refs_0_ = bf16[2048,7168]{1,0:T(8,128)(2,1)} custom-call(bf16[2048,7168]{1,0:T(8,128)(2,1)} %mlp_ring.1.src_ref), custom_call_target="tpu_custom_call" | custom-call | flops 30064771072 | bytes 29360128 | tf_op jit(solution)/shard_map/copy_rows/pallas_call | solution.py:357
  346.8 0.0 collective-permute-done.3.refs_7_
  346.8 0.0 collective-permute-done.2.refs_6_
  346.8 0.0 collective-permute-done.1.refs_2_
  346.8 0.0 collective-permute-done.refs_1_
  346.9 2.6 collective-permute-start.7
  349.6 0.0 collective-permute-start.6
  349.6 1.6 collective-permute-start.5
  351.2 0.0 collective-permute-start.4
  351.2 9.5 %copy_rows.3.refs_10_ = bf16[2048,7168]{1,0:T(8,128)(2,1)} custom-call(bf16[2048,7168]{1,0:T(8,128)(2,1)} %mlp_ring.1.src_ref, bf16[2048,7168]{1,0:T(8,128)(2,1)} %copy_rows.2.refs_0_), custom_call_target="tpu_custom_call", output_to_operand_aliasing={{}: (1, {})} | custom-call | flops 22548578304 | bytes 22020096 | tf_op jit(solution)/shard_map/copy_rows/pallas_call | solution.py:357
  360.7 0.0 collective-permute-done.7.refs_9_
  360.8 0.0 collective-permute-done.6.refs_8_
  360.8 0.0 collective-permute-done.5.refs_4_
  360.8 0.0 collective-permute-done.4.refs_3_
  360.8 1.9 place_pieces.1
  (4 shorter events, 0.1 us)
Async XLA Ops:
  329.6 17.2 %collective-permute-start.3 = (bf16[64,3584]{1,0:T(8,128)(2,1)S(1)}, bf16[64,3584]{1,0:T(8,128)(2,1)S(1)}, u32[]{:S(2)}, u32[]{:S(2)}) collective-permute-start(bf16[64,3584]{1,0:T(8,128)(2,1)S(1)} %get-tuple-element.15.refs_5_), channel_id=1, source_target_pairs={{0,3},{1,0},{2,1},{3,2},{4,7},{5,4},{6,5},{7,6},{8,11},{9,8},{10,9... | collective-permute-start | bytes 1376264 | tf_op jit(solution)/shard_map/ppermute | solution.py:427
  332.7 14.2 %collective-permute-start.2 = (bf16[64,3584]{1,0:T(8,128)(2,1)S(1)}, bf16[64,3584]{1,0:T(8,128)(2,1)S(1)}, u32[]{:S(2)}, u32[]{:S(2)}) collective-permute-start(bf16[64,3584]{1,0:T(8,128)(2,1)S(1)} %get-tuple-element.15.refs_5_), channel_id=1, source_target_pairs={{0,1},{1,2},{2,3},{3,0},{4,5},{5,6},{6,7},{7,4},{8,9},{9,10},{10,1... | collective-permute-start | bytes 1376264 | tf_op jit(solution)/shard_map/ppermute | solution.py:427
  332.7 14.2 %collective-permute-start.1 = (bf16[64,3584]{1,0:T(8,128)(2,1)S(1)}, bf16[64,3584]{1,0:T(8,128)(2,1)S(1)}, u32[]{:S(2)}, u32[]{:S(2)}) collective-permute-start(bf16[64,3584]{1,0:T(8,128)(2,1)S(1)} %get-tuple-element.16.refs_0_), channel_id=1, source_target_pairs={{0,12},{1,13},{2,14},{3,15},{4,0},{5,1},{6,2},{7,3},{8,4},{9,5},{1... | collective-permute-start | bytes 1376264 | tf_op jit(solution)/shard_map/ppermute | solution.py:427
  334.2 12.6 %collective-permute-start = (bf16[64,3584]{1,0:T(8,128)(2,1)S(1)}, bf16[64,3584]{1,0:T(8,128)(2,1)S(1)}, u32[]{:S(2)}, u32[]{:S(2)}) collective-permute-start(bf16[64,3584]{1,0:T(8,128)(2,1)S(1)} %get-tuple-element.16.refs_0_), channel_id=1, source_target_pairs={{0,4},{1,5},{2,6},{3,7},{4,8},{5,9},{6,10},{7,11},{8,12},{9,13},{1... | collective-permute-start | bytes 1376264 | tf_op jit(solution)/shard_map/ppermute | solution.py:427
  346.9 13.8 %collective-permute-start.7 = (bf16[64,1792]{1,0:T(8,128)(2,1)S(1)}, bf16[64,1792]{1,0:T(8,128)(2,1)S(1)}, u32[]{:S(2)}, u32[]{:S(2)}) collective-permute-start(bf16[64,1792]{1,0:T(8,128)(2,1)S(1)} %slice.15), channel_id=1, source_target_pairs={{0,3},{1,0},{2,1},{3,2},{4,7},{5,4},{6,5},{7,6},{8,11},{9,8},{10,9... | collective-permute-start | bytes 688136 | tf_op jit(solution)/shard_map/ppermute | solution.py:439
  349.6 11.2 %collective-permute-start.6 = (bf16[64,1792]{1,0:T(8,128)(2,1)S(1)}, bf16[64,1792]{1,0:T(8,128)(2,1)S(1)}, u32[]{:S(2)}, u32[]{:S(2)}) collective-permute-start(bf16[64,1792]{1,0:T(8,128)(2,1)S(1)} %slice.14), channel_id=1, source_target_pairs={{0,1},{1,2},{2,3},{3,0},{4,5},{5,6},{6,7},{7,4},{8,9},{9,10},{10,1... | collective-permute-start | bytes 688136 | tf_op jit(solution)/shard_map/ppermute | solution.py:438
  349.6 11.2 %collective-permute-start.5 = (bf16[64,1792]{1,0:T(8,128)(2,1)S(1)}, bf16[64,1792]{1,0:T(8,128)(2,1)S(1)}, u32[]{:S(2)}, u32[]{:S(2)}) collective-permute-start(bf16[64,1792]{1,0:T(8,128)(2,1)S(1)} %slice.13), channel_id=1, source_target_pairs={{0,12},{1,13},{2,14},{3,15},{4,0},{5,1},{6,2},{7,3},{8,4},{9,5},{1... | collective-permute-start | bytes 688136 | tf_op jit(solution)/shard_map/ppermute | solution.py:439
  351.2 9.6 %collective-permute-start.4 = (bf16[64,1792]{1,0:T(8,128)(2,1)S(1)}, bf16[64,1792]{1,0:T(8,128)(2,1)S(1)}, u32[]{:S(2)}, u32[]{:S(2)}) collective-permute-start(bf16[64,1792]{1,0:T(8,128)(2,1)S(1)} %slice.12), channel_id=1, source_target_pairs={{0,4},{1,5},{2,6},{3,7},{4,8},{5,9},{6,10},{7,11},{8,12},{9,13},{1... | collective-permute-start | bytes 688136 | tf_op jit(solution)/shard_map/ppermute | solution.py:438

commit v3 on v2

--- a/solution.py
+++ b/solution.py
@@ -14,14 +14,16 @@
 CHUNK = 256
 STREAMS = 8
 TILE = 128
-COPY_FLOPS = 4096
+COPY_ROWS = 128
+LOW_CHUNKS = 4
+LIMIT = 20 << 20
 GU_SLOTS = 3
 DN_SLOTS = 3
 
 
 def kernel(
     side,
-    x_hbm, wg_hbm, wu_hbm, wd_hbm, y_hbm,
+    x_hbm, wg_hbm, wu_hbm, wd_hbm, y_hbm, y_vmem,
     x_buf, gu_buf, dn_buf, hidden, part, xred, out1, in1, out2, in2, fin,
     x_sem, gu_sem, dn_sem, fin_sem,
     send1, recv1, send2, recv2, send3, recv3, send4, recv4,
@@ -62,9 +64,20 @@
     def y_rows(start, size):
         return pl.ds(pl.multiple_of(start, 16), size)
 
+    high = chunks - LOW_CHUNKS
+
+    def placed(j, f):
+        @pl.when(j < high)
+        def _():
+            f(y_hbm, j * CHUNK)
+
+        @pl.when(j >= high)
+        def _():
+            f(y_vmem, (j - high) * CHUNK)
+
     def x_copy(j):
         return pltpu.make_async_copy(
-            x_hbm.at[pl.ds(pl.multiple_of(j * CHUNK, CHUNK), CHUNK)], x_buf.at[j % 2], x_sem.at[j % 2]
+            x_hbm.at[pl.ds(pl.multiple_of(j * CHUNK, CHUNK), CHUNK)], x_buf, x_sem
         )
 
     def gu_copies(g):
@@ -90,7 +103,7 @@
 
             for c in gu_copies(g):
                 c.wait()
-            both = jnp.dot(x_buf[j % 2], gu_buf[g % GU_SLOTS], preferred_element_type=F32)
+            both = jnp.dot(x_buf[...], gu_buf[g % GU_SLOTS], preferred_element_type=F32)
             gate, up = both[:, :TILE], both[:, TILE:]
             hidden[u] = (jax.nn.silu(gate) * up).astype(BF16)
 
@@ -99,18 +112,14 @@
                 for c in gu_copies(g + GU_SLOTS):
                     c.start()
 
-            @pl.when((u == gu_units - 1) & (j + 2 < chunks))
-            def _():
-                x_copy(j + 2).start()
+            @pl.when((u == gu_units - 1) & (j + 1 < chunks))
+            def _():
+                x_copy(j + 1).start()
 
             @pl.when((j == 0) & (u == gu_units // 2))
             def _():
                 for i in range(DN_SLOTS):
                     dn_copy(i).start()
-
-            @pl.when((j == 0) & (u == gu_units - 1))
-            def _():
-                x_copy(1).start()
 
         @pl.when(u >= gu_units)
         def _():
@@ -138,21 +147,21 @@
         _, _, _, _, n2 = place(c)
         return remote(out2.at[k, c], in2.at[j % 2, k, c], send2.at[k, c], recv2.at[j % 2, k, c], n2)
 
-    def ag2(j, k, c, own):
+    def ag2(j, k, c, own, y=y_hbm, row=0):
         d, p1, p2, _, n2 = place(c)
         r = (p2 - d * k + 2 * side) % side
-        at = y_hbm.at[y_rows(j * CHUNK + p1 * piece + r * sub, sub), colour_cols(c)]
+        at = y.at[y_rows(row + p1 * piece + r * sub, sub), colour_cols(c)]
         return remote(fin.at[c] if own else at, at, send3.at[k, c], recv3.at[j % 2, k, c], n2)
 
-    def ag1(j, k, s):
+    def ag1(j, k, s, y=y_hbm, row=0):
         d, p1, _, n1, _ = place(s)
         q = (p1 - d * k + 2 * side) % side
-        at = y_hbm.at[y_rows(j * CHUNK + q * piece, piece), cols(s)]
+        at = y.at[y_rows(row + q * piece, piece), cols(s)]
         return remote(at, at, send4.at[k, s], recv4.at[j % 2, k, s], n1)
 
-    def fin_copy(j, c):
+    def fin_copy(c, y, row):
         _, p1, p2, _, _ = place(c)
-        at = y_hbm.at[y_rows(j * CHUNK + p1 * piece + p2 * sub, sub), colour_cols(c)]
+        at = y.at[y_rows(row + p1 * piece + p2 * sub, sub), colour_cols(c)]
         return pltpu.make_async_copy(fin.at[c], at, fin_sem.at[c])
 
     def each(first, count, f):
@@ -213,7 +222,7 @@
         @pl.when(k == 0)
         def _():
             def add(c):
-                _, _, p2, _, _ = place(c)
+                _, p1, p2, _, _ = place(c)
 
                 @pl.when(j > 0)
                 def _():
@@ -222,12 +231,20 @@
                 rs2(j, steps - 1, c).wait_recv()
                 for h in range(2):
                     mine = xred[j % 2, 4 * h + c, pl.ds(pl.multiple_of(p2 * sub, sub), sub), :]
-                    total = mine + in2[j % 2, steps - 1, c, h].astype(F32)
-                    fin[c, :, h * width : (h + 1) * width] = total.astype(BF16)
+                    total = (mine + in2[j % 2, steps - 1, c, h].astype(F32)).astype(BF16)
+                    fin[c, :, h * width : (h + 1) * width] = total
+
+                    @pl.when(j >= high)
+                    def _():
+                        at = y_rows((j - high) * CHUNK + p1 * piece + p2 * sub, sub)
+                        y_vmem[at, pl.ds(pl.multiple_of((2 * c + h) * width, 128), width)] = total
 
             def go(c):
-                ag2(j, 0, c, True).start()
-                fin_copy(j, c).start()
+                placed(j, lambda y, row: ag2(j, 0, c, True, y, row).start())
+
+                @pl.when(j < high)
+                def _():
+                    fin_copy(c, y_hbm, j * CHUNK).start()
 
             each(0, 4, add)
             each(0, 4, go)
@@ -239,12 +256,12 @@
                 def _():
                     ag2(j - 1, k, c, False).wait_send()
 
-                @pl.when(k == 1)
-                def _():
-                    fin_copy(j, c).wait()
+                @pl.when((k == 1) & (j < high))
+                def _():
+                    fin_copy(c, y_hbm, j * CHUNK).wait()
 
                 ag2(j, k - 1, c, False).wait_recv()
-                ag2(j, k, c, False).start()
+                placed(j, lambda y, row: ag2(j, k, c, False, y, row).start())
 
             each(0, 4, go)
 
@@ -268,7 +285,7 @@
             def _():
                 ag1(j, k - 1, s).wait_recv()
 
-            ag1(j, k, s).start()
+            placed(j, lambda y, row: ag1(j, k, s, y, row).start())
 
         each(4 * half, 4, go)
 
@@ -312,7 +329,7 @@
         def _():
             phase3(t - 2, k)
 
-        @pl.when((n >= fill) & (m >= 6) & (t >= 3) & (t - 3 < last))
+        @pl.when((n >= fill) & (m >= 6) & (t >= 3))
         def _():
             phase4(t - 3, k, half)
 
@@ -326,17 +343,16 @@
 
         return carry
 
-    lax.fori_loop(0, fill + (chunks + 2) * slots, turn, 0)
+    lax.fori_loop(0, fill + (chunks + 3) * slots, turn, 0)
 
     def drain(s, carry):
-        ag1(last - 1, steps - 1, s).wait_recv()
+        ag1(last, steps - 1, s).wait_recv()
         for k in range(steps):
             rs1(last, k, s).wait_send()
-            ag1(last - 1, k, s).wait_send()
+            ag1(last, k, s).wait_send()
         return carry
 
     def drain2(c, carry):
-        ag2(last, steps - 1, c, False).wait_recv()
         for k in range(steps):
             rs2(last, k, c).wait_send()
             ag2(last, k, c, k == 0).wait_send()
@@ -346,103 +362,60 @@
     lax.fori_loop(0, 4, drain2, 0)
 
 
-def copy_rows(src_ref, *refs):
-    refs[-1][...] = src_ref[...]
-
-
-def copy_into(src, dst, first, count, block):
-    rows, width = src.shape
-    at = first // block
-    spec = pl.BlockSpec((block, width), lambda i: (i + at, 0))
+def copy_kernel(high_ref, low_ref, out_ref, buf, load_sem, store_sem, direct_sem):
+    rows_low = low_ref.shape[0]
+    rows_high = high_ref.shape[0] - rows_low
+    n = rows_high // COPY_ROWS
+    slots = buf.shape[0]
+
+    def load(i):
+        return pltpu.make_async_copy(high_ref.at[pl.ds(i * COPY_ROWS, COPY_ROWS)], buf.at[i % slots], load_sem.at[i % slots])
+
+    def store(i):
+        return pltpu.make_async_copy(buf.at[i % slots], out_ref.at[pl.ds(i * COPY_ROWS, COPY_ROWS)], store_sem.at[i % slots])
+
+    pieces = rows_low // COPY_ROWS
+    direct = [
+        pltpu.make_async_copy(
+            low_ref.at[pl.ds(i * COPY_ROWS, COPY_ROWS)],
+            out_ref.at[pl.ds(rows_high + i * COPY_ROWS, COPY_ROWS)],
+            direct_sem.at[i],
+        )
+        for i in range(pieces)
+    ]
+    for i in range(min(slots, n)):
+        load(i).start()
+    for c in direct:
+        c.start()
+    for i in range(n):
+        load(i).wait()
+        store(i).start()
+        if i + slots < n:
+            store(i).wait()
+            load(i + slots).start()
+    for i in range(max(n - slots, 0), n):
+        store(i).wait()
+    for c in direct:
+        c.wait()
+
+
+def join(high, low):
+    rows, d_out = high.shape
+    slots = min(6, (rows - low.shape[0]) // COPY_ROWS)
     return pl.pallas_call(
-        copy_rows,
-        grid=(count // block,),
-        out_shape=jax.ShapeDtypeStruct(src.shape, src.dtype),
-        in_specs=[spec] + ([] if dst is None else [pl.BlockSpec(memory_space=pl.ANY)]),
-        out_specs=spec,
-        input_output_aliases={} if dst is None else {1: 0},
-        compiler_params=pltpu.CompilerParams(vmem_limit_bytes=44 << 20),
-        cost_estimate=pl.CostEstimate(
-            flops=count * width * COPY_FLOPS, bytes_accessed=4 * count * width, transcendentals=0
-        ),
-        name="copy_rows",
-    )(*([src] if dst is None else [src, dst]))
-
-
-def place_pieces(side, n_in, base, *refs):
-    ins, out, sems = refs[:n_in], refs[n_in + 1], refs[n_in + 2]
-    me = lax.axis_index("tp")
-    px, py = me // side, me % side
-    piece = ins[0].shape[0]
-    half, quarter = ins[0].shape[1], ins[0].shape[1] // 2
-    stores = []
-    for axis, p in enumerate((px, py)):
-        for n, (shift, col, w) in enumerate(
-            ((0, 0, half), (side - 1, 0, half), (1, 0, half), (side - 2, 0, quarter), (2, quarter, quarter))
-        ):
-            i = axis * 5 + n
-            at = pl.ds(pl.multiple_of(base + (p + shift) % side * piece, piece), piece)
-            stores.append(
-                pltpu.make_async_copy(ins[i], out.at[at, pl.ds(axis * half + col, w)], sems.at[i])
-            )
-    for store in stores:
-        store.start()
-    for store in stores:
-        store.wait()
-
-
-def finish(side, y, base, pieces):
-    n = len(pieces)
-    any_spec = pl.BlockSpec(memory_space=pl.ANY)
-    return pl.pallas_call(
-        functools.partial(place_pieces, side, n, base),
-        out_shape=jax.ShapeDtypeStruct(y.shape, y.dtype),
-        in_specs=[pl.BlockSpec(memory_space=pltpu.VMEM)] * n + [any_spec],
-        out_specs=any_spec,
-        scratch_shapes=[pltpu.SemaphoreType.DMA((n,))],
-        input_output_aliases={n: 0},
-        compiler_params=pltpu.CompilerParams(vmem_limit_bytes=8 << 20),
-        name="place_pieces",
-    )(*pieces, y)
-
-
-def gather_last(side, y):
-    rows, d_out = y.shape
-    half, quarter, piece, base = d_out // 2, d_out // 4, CHUNK // side, rows - CHUNK
-    me = lax.axis_index("tp")
-    px, py = me // side, me % side
-
-    def ring(dx, dy):
-        grid = [(x, w) for x in range(side) for w in range(side)]
-        return [(x * side + w, (x + dx) % side * side + (w + dy) % side) for x, w in grid]
-
-    pieces = []
-    near, own = [], []
-    for axis, p in enumerate((px, py)):
-        mine = lax.dynamic_slice(y, (base + p * piece, axis * half), (piece, half))
-        own.append(mine)
-    for axis in range(2):
-        step = (1, 0) if axis == 0 else (0, 1)
-        back = (-1, 0) if axis == 0 else (0, -1)
-        near.append((lax.ppermute(own[axis], "tp", ring(*step)), lax.ppermute(own[axis], "tp", ring(*back))))
-    part = base * 5 // 8 // 128 * 128
-    out = copy_into(y, None, 0, part, 128)
-    (near, out) = lax.optimization_barrier((near, out))
-    far = []
-    for axis in range(2):
-        step = (1, 0) if axis == 0 else (0, 1)
-        back = (-1, 0) if axis == 0 else (0, -1)
-        from_back, from_ahead = near[axis]
-        far.append(
-            (
-                lax.ppermute(from_back[:, :quarter], "tp", ring(*step)),
-                lax.ppermute(from_ahead[:, quarter:], "tp", ring(*back)),
-            )
-        )
-    out = copy_into(y, out, part, base - part, 128)
-    for axis in range(2):
-        pieces += [own[axis], *near[axis], *far[axis]]
-    return finish(side, out, base, pieces)
+        copy_kernel,
+        out_shape=jax.ShapeDtypeStruct((rows, d_out), BF16),
+        in_specs=[pl.BlockSpec(memory_space=pl.ANY), pl.BlockSpec(memory_space=pltpu.VMEM)],
+        out_specs=pl.BlockSpec(memory_space=pl.ANY),
+        scratch_shapes=[
+            pltpu.VMEM((slots, COPY_ROWS, d_out), BF16),
+            pltpu.SemaphoreType.DMA((slots,)),
+            pltpu.SemaphoreType.DMA((slots,)),
+            pltpu.SemaphoreType.DMA((low.shape[0] // COPY_ROWS,)),
+        ],
+        compiler_params=pltpu.CompilerParams(vmem_limit_bytes=LIMIT),
+        name="join",
+    )(high, low)
 
 
 def solution(mesh):
@@ -456,15 +429,19 @@
         piece = CHUNK // side
         sub = piece // side
         steps = side - 1
+        low = LOW_CHUNKS * CHUNK
         any_spec = pl.BlockSpec(memory_space=pl.ANY)
         dma = pltpu.SemaphoreType.DMA
         y = pl.pallas_call(
             functools.partial(kernel, side),
-            out_shape=jax.ShapeDtypeStruct((rows, d_out), BF16),
+            out_shape=(
+                jax.ShapeDtypeStruct((rows, d_out), BF16),
+                pltpu.VMEM((low, d_out), BF16),
+            ),
             in_specs=[any_spec] * 4,
-            out_specs=any_spec,
+            out_specs=(any_spec, pl.BlockSpec(memory_space=pltpu.VMEM)),
             scratch_shapes=[
-                pltpu.VMEM((2, CHUNK, depth), BF16),
+                pltpu.VMEM((CHUNK, depth), BF16),
                 pltpu.VMEM((GU_SLOTS, depth, 2 * TILE), BF16),
                 pltpu.VMEM((DN_SLOTS, ff, width), BF16),
                 pltpu.VMEM((ff // TILE, CHUNK, TILE), BF16),
@@ -475,21 +452,21 @@
                 pltpu.VMEM((steps, 4, 2, sub, width), BF16),
                 pltpu.VMEM((2, steps, 4, 2, sub, width), BF16),
                 pltpu.VMEM((4, sub, 2 * width), BF16),
-                dma((2,)),
+                dma,
                 dma((GU_SLOTS, 2)),
                 dma((DN_SLOTS,)),
                 dma((4,)),
             ]
             + [dma((steps, n)) if one else dma((2, steps, n)) for n in (8, 4, 4, 8) for one in (1, 0)],
             compiler_params=pltpu.CompilerParams(
-                collective_id=0, has_side_effects=True, vmem_limit_bytes=66_000_000
+                collective_id=0, has_side_effects=True, vmem_limit_bytes=51_900_000
             ),
             cost_estimate=pl.CostEstimate(
                 flops=6 * rows * depth * ff, bytes_accessed=8 * 3 * depth * ff * 2, transcendentals=rows * ff
             ),
             name="mlp_ring",
         )(x, w_gate, w_up, w_down)
-        return gather_last(side, y)
+        return join(*y)
 
     return jax.shard_map(
         step,

time: 364 us -> 359 us (0.986)
  starting transfers between devices: 8.87 us -> 0 us
  Pallas kernels: 352 us -> 359 us
    ppermute x8 -> x0, starting transfers between devices: 8.87 us -> none  [the longest x2 4.6 us: gather_last(): lax.ppermute(own[axis], 'tp', ring(*back))]
    pallas_call x4 -> x2, Pallas kernels: 352 us -> 359 us  [the longest x1 343 us: step(): pl.pallas_call(functools.partial(kernel, side), out_shape=(jax.ShapeDtype...]
  transfers between devices with their start and end apart: 8 -> 0, of which waited for: 0 -> 0; matrix products, arithmetic and copies ran while one was open for 0% -> 0% of each run, Pallas kernels for 6% -> 0%
where the time goes in v3:
time: 359 us
  Pallas kernels  359 us (100%)
    pallas_call x1, Pallas kernels, step(): pl.pallas_call(functools.partial(kernel, side), out_shape=(jax.ShapeDtype...  343 us
    pallas_call x1, Pallas kernels, join(): pl.pallas_call(copy_kernel, out_shape=jax.ShapeDtypeStruct((rows, d_out),...  16 us

profile of v3, /device:TPU:97, one launch (start us, length us, event | category | flops | bytes accessed | tf_op | source)
XLA Modules:
  0.0 358.9 jit_solution(8103171933797487195)
XLA Ops:
  0.0 343.0 %mlp_ring.1 = (bf16[2048,7168]{1,0:T(8,128)(2,1)}, bf16[1024,7168]{1,0:T(8,128)(2,1)S(1)}) custom-call(bf16[2048,7168]{1,0:T(8,128)(2,1)} %x_hbm.1, bf16[7168,1152]{1,0:T(8,128)(2,1)} %wg_hbm.1, bf16[7168,1152]{1,0:T(8,128)(2,1)} %wu_hbm.1, bf16[1152,7168]{1,0:T(8,128)(2,1)} %wd_hbm.1), custom_call_target="tpu_custom_call" | custom-call | flops 101468602368 | bytes 396361728 | tf_op jit(solution)/shard_map/mlp_ring/pallas_call | solution.py:435
  343.0 16.0 %join.1 = bf16[2048,7168]{1,0:T(8,128)(2,1)} custom-call(bf16[2048,7168]{1,0:T(8,128)(2,1)} %get-tuple-element.7.high_ref, bf16[1024,7168]{1,0:T(8,128)(2,1)S(1)} %get-tuple-element.8.low_ref), custom_call_target="tpu_custom_call" | custom-call | tf_op jit(solution)/shard_map/join/pallas_call | solution.py:405
